TPU v7x, 32 devices: a whole 2x2x4 slice. The times are simulated.
32 devices in a mesh: blk: 8 (over z, x), dp: 4 (over y, core).
Axes of the slice: x: 2, y: 2, z: 4, core: 2. Of those that a mesh axis runs over, the one named last changes fastest.
Arguments:
- tokens: bfloat16 [1024, 5120], P('blk', 'dp'), may hold values from -6 to 6
- expert_ids: int32 [1024, 6], P('blk'), may hold values from 0 to 15, all different within a row; in each aligned block of 128 rows (0 to 127, 128 to 255, ...) at most 96 rows name the same one
- gate_vals: float32 [1024, 6], P('blk'), may hold values from 0.1 to 1
- w_gate: bfloat16 [16, 5120, 1536], P('blk', 'dp'), may hold values from -0.078125 to 0.078125
- w_up: bfloat16 [16, 5120, 1536], P('blk', 'dp'), may hold values from -0.078125 to 0.078125
- w_down: bfloat16 [16, 5120, 1536], P('blk', 'dp'), may hold values from -0.15625 to 0.15625
Outputs:
- combined: bfloat16 [1024, 5120], P('blk', 'dp')
Inputs may be any that keep to these rules, and one draw needn't show every extreme that they name: `expert_ids`: each row names 6 different experts. Among the 128 rows of one index of blk (aligned blocks) no expert is named more than 96 times, a bound that some block reaches.
All inputs are finite; a program needn't handle non-finite values.
Results may differ from a plain program's by a relative error of at most 0.0057.
Values may be sent and summed in bfloat16 or wider, within the bound.
A program may use at most 128 MiB of HBM per device.

v0:
```python
import functools

import jax
import jax.numpy as jnp
from jax import lax
from jax.experimental import pallas as pl
from jax.experimental.pallas import tpu as pltpu
from jax.sharding import PartitionSpec as P

MESH = pl.DeviceIdType.MESH
VMEM_BYTES = 66_000_000


def flip(a, m, size):
    total, unit = 0, 1
    while unit < size:
        total = total + lax.rem(lax.div(a, unit) + lax.div(m, unit), 2) * unit
        unit *= 2
    return total


def fused_kernel(
    n_blk, tok_ref, info_ref, wg_hbm, wu_hbm, wd_hbm, out_ref,
    wg, wu, wd, everyone, routed, part, near, far_out, far_in, hidden, rows_out,
    outgoing, arrived, acc, info, high, low, hot,
    w_sem, tok_s, tok_r, near_s, near_r, far_s, far_r, hy_s, hy_r, hc_s, hc_r, hf_s, hf_r, ret_s, ret_r, info_s, info_r,
):
    blk = lax.axis_index("blk")
    dp = lax.axis_index("dp")
    y, c = lax.div(dp, 2), lax.rem(dp, 2)
    mate = (blk, y * 2 + (1 - c))
    across = (blk, (1 - y) * 2 + c)
    ff = wg.shape[2]
    width = wg.shape[1]
    half = part.shape[3]
    cap = 2 * half

    def copy(src, dst, send, recv, device):
        return pltpu.make_async_remote_copy(
            src_ref=src, dst_ref=dst, send_sem=send, recv_sem=recv,
            device_id=device, device_id_type=MESH,
        )

    def peer(m):
        return (flip(blk, m, n_blk), dp)

    def mask_of(i):
        m = jnp.where(i == 0, 0, jnp.where(i == 1, 2, i + 2))
        return jnp.where(i == n_blk - 2, 3, jnp.where(i == n_blk - 1, 1, m))

    def tok_direct(m):
        return copy(tok_ref, everyone.at[m], tok_s.at[m], tok_r.at[m], peer(m))

    def info_direct(m):
        return copy(info_ref, info.at[m], info_s.at[m], info_r.at[m], peer(m))

    def tok_onward(m):
        return copy(everyone.at[m], everyone.at[m + 1], tok_s.at[m + 1], tok_r.at[m + 1], peer(1))

    def near_copy(j):
        return copy(part.at[lax.rem(j, 2), 1 - c], near.at[j], near_s.at[j], near_r.at[j], mate)

    def far_copy(j):
        return copy(far_out.at[j], far_in.at[j], far_s.at[j], far_r.at[j], across)

    def hidden_far(j):
        return copy(hidden.at[j, y, c], hidden.at[j, y, c], hy_s.at[j], hy_r.at[j], across)

    def hidden_near(j):
        return copy(hidden.at[j, y, c], hidden.at[j, y, c], hc_s.at[j], hc_r.at[j], mate)

    def hidden_onward(j):
        return copy(hidden.at[j, 1 - y, c], hidden.at[j, 1 - y, c], hf_s.at[j], hf_r.at[j], mate)

    def ret_copy(m):
        return copy(outgoing.at[m], arrived.at[m], ret_s.at[m], ret_r.at[m], peer(m))

    loads = [
        pltpu.make_async_copy(wg_hbm, wg, w_sem.at[0]),
        pltpu.make_async_copy(wu_hbm, wu, w_sem.at[1]),
        pltpu.make_async_copy(wd_hbm, wd, w_sem.at[2]),
    ]
    for load in loads:
        load.start()

    barrier = pltpu.get_barrier_semaphore()
    for m in range(1, n_blk):
        pl.semaphore_signal(barrier, inc=1, device_id=peer(m), device_id_type=MESH)
    for device in (mate, across):
        pl.semaphore_signal(barrier, inc=1, device_id=device, device_id_type=MESH)
    pl.semaphore_wait(barrier, n_blk + 1)

    for m in range(1, n_blk):
        info_direct(m).start()
    for m in [1] + list(range(2, n_blk, 2)):
        tok_direct(m).start()
    everyone[0] = tok_ref[...]
    info[0] = info_ref[...]
    tok_rows = tok_ref.shape[0]
    lines = info_ref.shape[0] // 2

    def slots_of(m):
        square = (tok_rows, tok_rows)
        before = lax.broadcasted_iota(jnp.int32, square, 0) < lax.broadcasted_iota(jnp.int32, square, 1)
        before = jnp.where(before, 1.0, 0.0).astype(jnp.bfloat16)
        slot = lax.broadcasted_iota(jnp.int32, (cap, tok_rows), 0).astype(jnp.float32)
        ids, gates = info[m, :lines], info[m, lines:]
        for h in range(2):
            match = ids == (2 * blk + h).astype(jnp.float32)
            member = jnp.sum(jnp.where(match, 1.0, 0.0), axis=0, keepdims=True)
            weight = jnp.sum(jnp.where(match, gates, 0.0), axis=0, keepdims=True)
            wide = jnp.broadcast_to(member, (16, tok_rows)).astype(jnp.bfloat16)
            position = jnp.dot(wide, before, preferred_element_type=jnp.float32)[0:1]
            taken = (slot == position) & (member > 0.5)
            weighted = jnp.where(taken, weight, 0.0)
            top = weighted.astype(jnp.bfloat16)
            span = slice(h * cap, (h + 1) * cap)
            high[m, span, :] = top
            low[m, span, :] = (weighted - top.astype(jnp.float32)).astype(jnp.bfloat16)
            hot[span, :] = jnp.where(taken, 1.0, 0.0).astype(jnp.bfloat16)

    def project(i):
        m = mask_of(i)

        @pl.when(i > 0)
        def _():
            info_direct(m).wait_recv()
            tok_direct(m).wait_recv()

        @pl.when((m > 0) & (lax.rem(m, 2) == 0))
        def _():
            tok_onward(m).start()

        slots_of(m)
        routed[...] = jnp.dot(
            hot[...], everyone[m], preferred_element_type=jnp.float32
        ).astype(jnp.bfloat16)

        @pl.when(i == 0)
        def _():
            loads[0].wait()
            loads[1].wait()

        slot = lax.rem(i, 2)
        tile = ff // 3 if ff % 384 == 0 else ff
        for h in range(2):
            rows = routed[h * cap:(h + 1) * cap, :]
            for which, w in enumerate((wg, wu)):
                for f in range(0, ff, tile):
                    got = jnp.dot(rows, w[h, :, f:f + tile], preferred_element_type=jnp.float32)
                    at = which * ff + f
                    part[slot, 0, h, :, at:at + tile] = got[:half]
                    part[slot, 1, h, :, at:at + tile] = got[half:]
        near_copy(i).start()

    def join(j):
        near_copy(j).wait()
        slot = lax.rem(j, 2)
        far_out[j] = (part[slot, c, 1 - y] + near[j, 1 - y]).astype(jnp.bfloat16)
        far_copy(j).start()
        near[j, y] = near[j, y] + part[slot, c, y]

    def activate(j):
        far_copy(j).wait_recv()
        gate = near[j, y, :, :ff] + far_in[j, :, :ff].astype(jnp.float32)
        up = near[j, y, :, ff:] + far_in[j, :, ff:].astype(jnp.float32)
        hidden[j, y, c] = (gate / (1.0 + jnp.exp(-gate)) * up).astype(jnp.bfloat16)
        hidden_far(j).start()
        hidden_near(j).start()

    def relay(j):
        hidden_far(j).wait_recv()
        hidden_onward(j).start()

    def finish(j):
        @pl.when(j == 0)
        def _():
            loads[2].wait()

        hidden_near(j).wait_recv()
        hidden_onward(j).wait_recv()
        m = mask_of(j)
        tile = 256 if width % 256 == 0 else width
        for h in range(2):
            rows = hidden[j, h].reshape(cap, ff)
            for d in range(0, width, tile):
                rows_out[h * cap:(h + 1) * cap, d:d + tile] = lax.dot_general(
                    rows, wd[h, d:d + tile, :], (((1,), (1,)), ((), ())),
                    preferred_element_type=jnp.float32,
                ).astype(jnp.bfloat16)
        over_slots = (((0,), (0,)), ((), ()))
        mixed = lax.dot_general(high[m], rows_out[...], over_slots, preferred_element_type=jnp.float32)
        mixed = mixed + lax.dot_general(
            low[m], rows_out[...], over_slots, preferred_element_type=jnp.float32
        )

        @pl.when(m == 0)
        def _():
            acc[...] = mixed

        @pl.when(m > 0)
        def _():
            outgoing[m] = mixed.astype(jnp.bfloat16)
            ret_copy(m).start()

    stages = ((1, join), (2, activate), (0, project), (3, relay), (4, finish))

    def step(i, carry):
        for lag, stage in stages:
            @pl.when((i >= lag) & (i - lag < n_blk))
            def _():
                stage(i - lag)
        return carry

    lax.fori_loop(0, n_blk + len(stages) - 1, step, 0)

    def gather_in(m, carry):
        ret_copy(m).wait_recv()
        acc[...] += arrived[m].astype(jnp.float32)
        return carry

    lax.fori_loop(1, n_blk, gather_in, 0)
    out_ref[...] = acc[...].astype(jnp.bfloat16)

    def drain(m, carry):
        far_copy(m).wait_send()
        hidden_far(m).wait_send()
        hidden_near(m).wait_send()
        hidden_onward(m).wait_send()

        @pl.when(m > 0)
        def _():
            info_direct(m).wait_send()
            tok_direct(m).wait_send()
            ret_copy(m).wait_send()

        return carry

    lax.fori_loop(0, n_blk, drain, 0)


def fused(tokens, expert_ids, gate_vals, w_gate, w_up, w_down):
    n_blk = lax.axis_size("blk")
    tok_rows, width = tokens.shape
    held, _, ff = w_gate.shape
    capacity = 2 * tok_rows * expert_ids.shape[1] // (held * n_blk)
    slots, half = held * capacity, capacity // 2
    top_k = expert_ids.shape[1]
    spare = ((0, -top_k % 8), (0, 0))
    ids = jnp.pad(expert_ids.T.astype(jnp.float32), spare, constant_values=-1.0)
    packed = jnp.concatenate((ids, jnp.pad(gate_vals.T, spare)), axis=0)
    bf, f32 = jnp.bfloat16, jnp.float32
    sems = [pltpu.SemaphoreType.DMA((n_blk,)) for _ in range(16)]
    vmem = pl.BlockSpec(memory_space=pltpu.VMEM)
    anywhere = pl.BlockSpec(memory_space=pl.ANY)
    return pl.pallas_call(
        functools.partial(fused_kernel, n_blk),
        out_shape=jax.ShapeDtypeStruct((tok_rows, width), bf),
        in_specs=[vmem] * 2 + [anywhere] * 3,
        out_specs=vmem,
        scratch_shapes=[
            pltpu.VMEM(w_gate.shape, bf),
            pltpu.VMEM(w_up.shape, bf),
            pltpu.VMEM(w_down.shape, bf),
            pltpu.VMEM((n_blk, tok_rows, width), bf),
            pltpu.VMEM((slots, width), bf),
            pltpu.VMEM((2, 2, held, half, 2 * ff), f32),
            pltpu.VMEM((n_blk, held, half, 2 * ff), f32),
            pltpu.VMEM((n_blk, half, 2 * ff), bf),
            pltpu.VMEM((n_blk, half, 2 * ff), bf),
            pltpu.VMEM((n_blk, held, 2, half, ff), bf),
            pltpu.VMEM((slots, width), bf),
            pltpu.VMEM((n_blk, tok_rows, width), bf),
            pltpu.VMEM((n_blk, tok_rows, width), bf),
            pltpu.VMEM((tok_rows, width), f32),
            pltpu.VMEM((n_blk,) + packed.shape, f32),
            pltpu.VMEM((n_blk, slots, tok_rows), bf),
            pltpu.VMEM((n_blk, slots, tok_rows), bf),
            pltpu.VMEM((slots, tok_rows), bf),
            pltpu.SemaphoreType.DMA((3,)),
        ] + sems,
        compiler_params=pltpu.CompilerParams(
            collective_id=0, has_side_effects=True, vmem_limit_bytes=VMEM_BYTES
        ),
    )(tokens, packed, w_gate, w_up, w_down)


def routing(expert_ids, gate_vals, held_count, capacity):
    first = lax.axis_index("blk") * held_count
    top_k = expert_ids.shape[1]
    both = jnp.concatenate((expert_ids.astype(jnp.float32), gate_vals), axis=1)
    both = lax.all_gather(both, "blk", axis=0, tiled=False)
    ids, gates = both[:, :, :top_k].astype(jnp.int32), both[:, :, top_k:]
    mine = first + jnp.arange(held_count, dtype=jnp.int32)
    match = ids[:, None, :, :] == mine[None, :, None, None]
    member = jnp.any(match, axis=3)
    weight = jnp.sum(jnp.where(match, gates[:, None], 0.0), axis=3)
    tok_rows = ids.shape[1]
    earlier = jnp.triu(jnp.ones((tok_rows, tok_rows), jnp.float32), 1)
    position = jnp.einsum(
        "bht,tu->bhu", member.astype(jnp.bfloat16), earlier.astype(jnp.bfloat16),
        preferred_element_type=jnp.float32,
    )
    slots = jnp.arange(capacity, dtype=jnp.int32).astype(jnp.float32)
    hot = member[:, :, None, :] & (position[:, :, None, :] == slots[None, None, :, None])
    return hot.astype(jnp.bfloat16), jnp.where(hot, weight[:, :, None, :], 0.0)


def local(tokens, expert_ids, gate_vals, w_gate, w_up, w_down):
    blk_size = lax.axis_size("blk")
    tok_rows, width_dev = tokens.shape
    top_k = expert_ids.shape[1]
    held_count = w_gate.shape[0]
    capacity = 2 * tok_rows * top_k // (held_count * blk_size)
    hot, weighted = routing(expert_ids, gate_vals, held_count, capacity)
    everyone = lax.all_gather(tokens, "blk", axis=0, tiled=False)
    routed = jnp.einsum("bhpt,btd->hbpd", hot, everyone, preferred_element_type=jnp.float32)
    routed = routed.astype(jnp.bfloat16).reshape(held_count, blk_size * capacity, width_dev)
    gate_part = jnp.einsum("emd,edf->emf", routed, w_gate, preferred_element_type=jnp.float32)
    up_part = jnp.einsum("emd,edf->emf", routed, w_up, preferred_element_type=jnp.float32)
    both = jnp.stack((gate_part, up_part), axis=0)
    summed = lax.psum_scatter(both, "dp", scatter_dimension=2, tiled=True)
    hidden = (jax.nn.silu(summed[0]) * summed[1]).astype(jnp.bfloat16)
    hidden = lax.all_gather(hidden, "dp", axis=1, tiled=True)
    result = jnp.einsum("emf,edf->emd", hidden, w_down, preferred_element_type=jnp.float32)
    result = result.astype(jnp.bfloat16).reshape(held_count, blk_size, capacity, width_dev)
    high = weighted.astype(jnp.bfloat16)
    low = (weighted - high.astype(jnp.float32)).astype(jnp.bfloat16)
    partial = jnp.einsum(
        "bhpt,hbpd->btd", high, result, preferred_element_type=jnp.float32
    ) + jnp.einsum("bhpt,hbpd->btd", low, result, preferred_element_type=jnp.float32)
    partial = partial.astype(jnp.bfloat16).reshape(blk_size * tok_rows, width_dev)
    return lax.psum_scatter(partial, "blk", scatter_dimension=0, tiled=True)


def choose(tokens, expert_ids, gate_vals, w_gate, w_up, w_down):
    n_blk, held = lax.axis_size("blk"), w_gate.shape[0]
    capacity = 2 * tokens.shape[0] * expert_ids.shape[1] // (held * n_blk)
    fits = lax.axis_size("dp") == 4 and held == 2 and n_blk == 8 and capacity % 32 == 0
    body = fused if fits else local
    return body(tokens, expert_ids, gate_vals, w_gate, w_up, w_down)


def solution(mesh):
    return jax.shard_map(
        choose,
        mesh=mesh,
        in_specs=(
            P("blk", "dp"),
            P("blk", None),
            P("blk", None),
            P("blk", "dp", None),
            P("blk", "dp", None),
            P("blk", "dp", None),
        ),
        out_specs=P("blk", "dp"),
        check_vma=False,
    )
```

profile of v0, /device:TPU:0, one launch (start us, length us, event | category | flops | bytes accessed | tf_op | source)
XLA Modules:
  0.0 129.6 jit_solution(12972934163855700128)
XLA Ops:
  0.0 0.7 convert_bitcast_fusion
  0.7 1.3 select_maximum_fusion.info_ref
  2.0 125.9 %shard_map.64 = bf16[128,1280]{1,0:T(8,128)(2,1)} custom-call(bf16[128,1280]{1,0:T(8,128)(2,1)} %tok_ref.1, f32[16,128]{1,0:T(8,128)} %select_maximum_fusion.info_ref, bf16[2,1280,1536]{2,1,0:T(8,128)(2,1)} %wg_hbm.1, bf16[2,1280,1536]{2,1,0:T(8,128)(2,1)} %wu_hbm.1, bf16[2,1280,1536]{2,1,0:T(8,128)(2,1)} %wd_hbm.1), custom_call_target="tpu_custom_call" | custom-call | tf_op jit(solution)/shard_map/pallas_call | solution.py:256
  127.9 1.7 %copy.8 = bf16[128,1280]{1,0:T(8,128)(2,1)} copy(bf16[128,1280]{1,0:T(8,128)(2,1)} %shard_map.64) | data formatting | bytes 655360
where the time goes:
time: 130 us
  Pallas kernels  126 us (97%)
  other arithmetic  1.98 us (2%)
  local copies, waits for them, and re-layouts  1.72 us (1%)
    pallas_call x1, Pallas kernels, fused(): pl.pallas_call(functools.partial(fused_kernel, n_blk), out_shape=jax.Shap...  126 us

commit v1 on v0

v1 whole, which is shorter than its diff:
```python
import functools

import jax
import jax.numpy as jnp
from jax import lax
from jax.experimental import pallas as pl
from jax.experimental.pallas import tpu as pltpu
from jax.sharding import PartitionSpec as P

MESH = pl.DeviceIdType.MESH
VMEM_BYTES = 66_000_000
TILE = 384
DOWN = 256


def flip(a, m, size):
    total, unit = 0, 1
    while unit < size:
        total = total + lax.rem(lax.div(a, unit) + lax.div(m, unit), 2) * unit
        unit *= 2
    return total


def fused_kernel(
    n_blk, tok_ref, info_ref, wg_hbm, wu_hbm, wd_hbm, out_ref,
    wg, wu, wd, everyone, routed, part, near, far_out, far_in, hidden, rows_out,
    outgoing, arrived, hold, acc, info, high, low, hot,
    w_sem, tok_s, tok_r, near_s, near_r, far_s, far_r, hy_s, hy_r, hc_s, hc_r, hf_s, hf_r, ret_s, ret_r, info_s, info_r,
):
    blk = lax.axis_index("blk")
    dp = lax.axis_index("dp")
    y, c = lax.div(dp, 2), lax.rem(dp, 2)
    mate = (blk, y * 2 + (1 - c))
    across = (blk, (1 - y) * 2 + c)
    held, width, ff = wg.shape
    cols = ff // 2
    half = near.shape[2]
    cap = 2 * half
    units = held * n_blk

    def copy(src, dst, send, recv, device):
        return pltpu.make_async_remote_copy(
            src_ref=src, dst_ref=dst, send_sem=send, recv_sem=recv,
            device_id=device, device_id_type=MESH,
        )

    def peer(m):
        return (flip(blk, m, n_blk), dp)

    def mask_of(i):
        m = jnp.where(i == 0, 0, jnp.where(i == 1, 2, i + 2))
        return jnp.where(i == n_blk - 2, 3, jnp.where(i == n_blk - 1, 1, m))

    def tok_direct(m):
        return copy(tok_ref, everyone.at[m], tok_s.at[m], tok_r.at[m], peer(m))

    def info_direct(m):
        return copy(info_ref, info.at[m], info_s.at[m], info_r.at[m], peer(m))

    def tok_onward(m):
        return copy(everyone.at[m], everyone.at[m + 1], tok_s.at[m + 1], tok_r.at[m + 1], peer(1))

    def near_copy(u):
        return copy(part.at[0], near.at[u], near_s.at[u], near_r.at[u], mate)

    def far_copy(u):
        return copy(far_out.at[u], far_in.at[u], far_s.at[u], far_r.at[u], across)

    def hidden_far(u):
        return copy(hidden.at[u, c, y], hidden.at[u, c, y], hy_s.at[u], hy_r.at[u], across)

    def hidden_near(u):
        return copy(hidden.at[u, c, y], hidden.at[u, c, y], hc_s.at[u], hc_r.at[u], mate)

    def hidden_onward(u):
        return copy(hidden.at[u, c, 1 - y], hidden.at[u, c, 1 - y], hf_s.at[u], hf_r.at[u], mate)

    def ret_copy(m):
        to = jnp.where(lax.rem(m, 2) == 1, 1, m)
        return copy(outgoing.at[m], arrived.at[m], ret_s.at[m], ret_r.at[m], peer(to))

    def load(k, h):
        hbm, vmem = ((wg_hbm, wg), (wu_hbm, wu), (wd_hbm, wd))[k]
        return pltpu.make_async_copy(hbm.at[h], vmem.at[h], w_sem.at[k, h])

    load(0, 0).start()
    load(1, 0).start()

    barrier = pltpu.get_barrier_semaphore()
    for m in range(1, n_blk):
        pl.semaphore_signal(barrier, inc=1, device_id=peer(m), device_id_type=MESH)
    for device in (mate, across):
        pl.semaphore_signal(barrier, inc=1, device_id=device, device_id_type=MESH)
    pl.semaphore_wait(barrier, n_blk + 1)

    for m in range(1, n_blk):
        info_direct(m).start()
    for m in [1] + list(range(2, n_blk - 2, 2)):
        tok_direct(m).start()
    everyone[0] = tok_ref[...]
    info[0] = info_ref[...]
    tok_rows = tok_ref.shape[0]
    lines = info_ref.shape[0] // 2

    def slots_of(m):
        square = (tok_rows, tok_rows)
        before = lax.broadcasted_iota(jnp.int32, square, 0) < lax.broadcasted_iota(jnp.int32, square, 1)
        before = jnp.where(before, 1.0, 0.0).astype(jnp.bfloat16)
        slot = lax.broadcasted_iota(jnp.int32, (cap, tok_rows), 0).astype(jnp.float32)
        ids, gates = info[m, :lines], info[m, lines:]
        for h in range(held):
            match = ids == (held * blk + h).astype(jnp.float32)
            member = jnp.sum(jnp.where(match, 1.0, 0.0), axis=0, keepdims=True)
            weight = jnp.sum(jnp.where(match, gates, 0.0), axis=0, keepdims=True)
            wide = jnp.broadcast_to(member, (16, tok_rows)).astype(jnp.bfloat16)
            position = jnp.dot(wide, before, preferred_element_type=jnp.float32)[0:1]
            taken = (slot == position) & (member > 0.5)
            weighted = jnp.where(taken, weight, 0.0)
            top = weighted.astype(jnp.bfloat16)
            span = slice(h * cap, (h + 1) * cap)
            high[m, span, :] = top
            low[m, span, :] = (weighted - top.astype(jnp.float32)).astype(jnp.bfloat16)
            hot[h] = jnp.where(taken, 1.0, 0.0).astype(jnp.bfloat16)

    def project(u):
        i, h = lax.div(u, held), lax.rem(u, held)
        m = mask_of(i)

        @pl.when(h == 0)
        def _():
            @pl.when(i > 0)
            def _():
                info_direct(m).wait_recv()

                @pl.when((lax.rem(m, 2) == 1) | (m == 2))
                def _():
                    tok_direct(m).wait_recv()

                @pl.when(m == 2)
                def _():
                    tok_onward(m).start()

            slots_of(m)

        routed[...] = jnp.dot(
            hot[h], everyone[m], preferred_element_type=jnp.float32
        ).astype(jnp.bfloat16)

        @pl.when(i == 0)
        def _():
            load(0, h).wait()
            load(1, h).wait()

            @pl.when(h == 0)
            def _():
                load(0, 1).start()
                load(1, 1).start()

            @pl.when(h == 1)
            def _():
                load(2, 0).start()
                load(2, 1).start()

        for side in range(2):
            first = jnp.where(c == side, cols, 0)
            for which, w in enumerate((wg, wu)):
                for f in range(0, cols, TILE):
                    at = pl.multiple_of(first + f, 128)
                    got = jnp.dot(
                        routed[...], w[h, :, pl.ds(at, TILE)], preferred_element_type=jnp.float32
                    )
                    span = slice(which * cols + f, which * cols + f + TILE)
                    part[side, 0, :, span] = got[:half]
                    part[side, 1, :, span] = got[half:]
            if side == 0:
                near_copy(u).start()

    def join(u):
        near_copy(u).wait()
        far_out[u] = (part[1, 1 - y] + near[u, 1 - y]).astype(jnp.bfloat16)
        far_copy(u).start()
        near[u, y] = near[u, y] + part[1, y]

    def activate(u):
        far_copy(u).wait_recv()
        gate = near[u, y, :, :cols] + far_in[u, :, :cols].astype(jnp.float32)
        up = near[u, y, :, cols:] + far_in[u, :, cols:].astype(jnp.float32)
        hidden[u, c, y] = (gate / (1.0 + jnp.exp(-gate)) * up).astype(jnp.bfloat16)
        hidden_far(u).start()
        hidden_near(u).start()

    def relay(u):
        hidden_far(u).wait_recv()
        hidden_onward(u).start()

    def finish(u):
        i, h = lax.div(u, held), lax.rem(u, held)
        m = mask_of(i)

        @pl.when(i == 0)
        def _():
            load(2, h).wait()

        hidden_near(u).wait_recv()
        hidden_onward(u).wait_recv()
        rows = jnp.concatenate([hidden[u, k].reshape(cap, cols) for k in range(2)], axis=1)
        for d in range(0, width, DOWN):
            rows_out[h, :, d:d + DOWN] = lax.dot_general(
                rows, wd[h, d:d + DOWN, :], (((1,), (1,)), ((), ())),
                preferred_element_type=jnp.float32,
            ).astype(jnp.bfloat16)

        @pl.when(h == held - 1)
        def _():
            both = rows_out[...].reshape(held * cap, width)
            over_slots = (((0,), (0,)), ((), ()))
            mixed = lax.dot_general(high[m], both, over_slots, preferred_element_type=jnp.float32)
            mixed = mixed + lax.dot_general(
                low[m], both, over_slots, preferred_element_type=jnp.float32
            )

            @pl.when(m == 0)
            def _():
                acc[...] = mixed

            @pl.when((m > 0) & (lax.rem(m, 2) == 0))
            def _():
                hold[lax.div(m, 2) - 1] = mixed

            @pl.when(lax.rem(m, 2) == 1)
            def _():
                outgoing[m] = mixed.astype(jnp.bfloat16)
                ret_copy(m).start()

    def spread(u):
        @pl.when(u == 3)
        def _():
            tok_direct(n_blk - 2).start()

        m = mask_of(jnp.minimum(lax.div(u + 1, held), n_blk - 1))

        @pl.when((lax.rem(u, held) == held - 1) & (m > 2) & (lax.rem(m, 2) == 0))
        def _():
            tok_direct(m).wait_recv()
            tok_onward(m).start()

    def merge(u):
        i = lax.div(u, held)
        m = mask_of(jnp.maximum(i - 1, 0)) - 1

        @pl.when((lax.rem(u, held) == held - 1) & (m > 0) & (lax.rem(m, 2) == 0))
        def _():
            ret_copy(m + 1).wait_recv()
            outgoing[m] = (hold[lax.div(m, 2) - 1] + arrived[m + 1].astype(jnp.float32)).astype(jnp.bfloat16)
            ret_copy(m).start()

    stages = ((1, join), (0, project), (2, activate), (3, relay), (4, finish), (0, spread), (4, merge))

    def step(s, carry):
        for lag, stage in stages:
            @pl.when((s >= lag) & (s - lag < units))
            def _():
                stage(s - lag)
        return carry

    lax.fori_loop(0, units + 4, step, 0)

    for m in [4, 6, 1, 2]:
        ret_copy(m).wait_recv()
        acc[...] += arrived[m].astype(jnp.float32)
    out_ref[...] = acc[...].astype(jnp.bfloat16)

    def drain(u, carry):
        far_copy(u).wait_send()
        hidden_far(u).wait_send()
        hidden_near(u).wait_send()
        hidden_onward(u).wait_send()
        return carry

    def drain_blocks(m, carry):
        info_direct(m).wait_send()
        tok_direct(m).wait_send()
        ret_copy(m).wait_send()
        return carry

    lax.fori_loop(0, units, drain, 0)
    lax.fori_loop(1, n_blk, drain_blocks, 0)


def fused(tokens, expert_ids, gate_vals, w_gate, w_up, w_down):
    n_blk = lax.axis_size("blk")
    tok_rows, width = tokens.shape
    held, _, ff = w_gate.shape
    capacity = 2 * tok_rows * expert_ids.shape[1] // (held * n_blk)
    half, units = capacity // 2, held * n_blk
    top_k = expert_ids.shape[1]
    spare = ((0, -top_k % 8), (0, 0))
    ids = jnp.pad(expert_ids.T.astype(jnp.float32), spare, constant_values=-1.0)
    packed = jnp.concatenate((ids, jnp.pad(gate_vals.T, spare)), axis=0)
    bf, f32 = jnp.bfloat16, jnp.float32
    dma = pltpu.SemaphoreType.DMA
    counts = [n_blk] * 2 + [units] * 10 + [n_blk] * 4
    vmem = pl.BlockSpec(memory_space=pltpu.VMEM)
    anywhere = pl.BlockSpec(memory_space=pl.ANY)
    return pl.pallas_call(
        functools.partial(fused_kernel, n_blk),
        out_shape=jax.ShapeDtypeStruct((tok_rows, width), bf),
        in_specs=[vmem] * 2 + [anywhere] * 3,
        out_specs=vmem,
        scratch_shapes=[
            pltpu.VMEM(w_gate.shape, bf),
            pltpu.VMEM(w_up.shape, bf),
            pltpu.VMEM(w_down.shape, bf),
            pltpu.VMEM((n_blk, tok_rows, width), bf),
            pltpu.VMEM((capacity, width), bf),
            pltpu.VMEM((2, 2, half, ff), f32),
            pltpu.VMEM((units, 2, half, ff), f32),
            pltpu.VMEM((units, half, ff), bf),
            pltpu.VMEM((units, half, ff), bf),
            pltpu.VMEM((units, 2, 2, half, ff // 2), bf),
            pltpu.VMEM((held, capacity, width), bf),
            pltpu.VMEM((n_blk, tok_rows, width), bf),
            pltpu.VMEM((n_blk, tok_rows, width), bf),
            pltpu.VMEM((n_blk // 2 - 1, tok_rows, width), f32),
            pltpu.VMEM((tok_rows, width), f32),
            pltpu.VMEM((n_blk,) + packed.shape, f32),
            pltpu.VMEM((n_blk, held * capacity, tok_rows), bf),
            pltpu.VMEM((n_blk, held * capacity, tok_rows), bf),
            pltpu.VMEM((held, capacity, tok_rows), bf),
            dma((3, held)),
        ] + [dma((count,)) for count in counts],
        compiler_params=pltpu.CompilerParams(
            collective_id=0, has_side_effects=True, vmem_limit_bytes=VMEM_BYTES
        ),
    )(tokens, packed, w_gate, w_up, w_down)


def routing(expert_ids, gate_vals, held_count, capacity):
    first = lax.axis_index("blk") * held_count
    top_k = expert_ids.shape[1]
    both = jnp.concatenate((expert_ids.astype(jnp.float32), gate_vals), axis=1)
    both = lax.all_gather(both, "blk", axis=0, tiled=False)
    ids, gates = both[:, :, :top_k].astype(jnp.int32), both[:, :, top_k:]
    mine = first + jnp.arange(held_count, dtype=jnp.int32)
    match = ids[:, None, :, :] == mine[None, :, None, None]
    member = jnp.any(match, axis=3)
    weight = jnp.sum(jnp.where(match, gates[:, None], 0.0), axis=3)
    tok_rows = ids.shape[1]
    earlier = jnp.triu(jnp.ones((tok_rows, tok_rows), jnp.float32), 1)
    position = jnp.einsum(
        "bht,tu->bhu", member.astype(jnp.bfloat16), earlier.astype(jnp.bfloat16),
        preferred_element_type=jnp.float32,
    )
    slots = jnp.arange(capacity, dtype=jnp.int32).astype(jnp.float32)
    hot = member[:, :, None, :] & (position[:, :, None, :] == slots[None, None, :, None])
    return hot.astype(jnp.bfloat16), jnp.where(hot, weight[:, :, None, :], 0.0)


def local(tokens, expert_ids, gate_vals, w_gate, w_up, w_down):
    blk_size = lax.axis_size("blk")
    tok_rows, width_dev = tokens.shape
    top_k = expert_ids.shape[1]
    held_count = w_gate.shape[0]
    capacity = 2 * tok_rows * top_k // (held_count * blk_size)
    hot, weighted = routing(expert_ids, gate_vals, held_count, capacity)
    everyone = lax.all_gather(tokens, "blk", axis=0, tiled=False)
    routed = jnp.einsum("bhpt,btd->hbpd", hot, everyone, preferred_element_type=jnp.float32)
    routed = routed.astype(jnp.bfloat16).reshape(held_count, blk_size * capacity, width_dev)
    gate_part = jnp.einsum("emd,edf->emf", routed, w_gate, preferred_element_type=jnp.float32)
    up_part = jnp.einsum("emd,edf->emf", routed, w_up, preferred_element_type=jnp.float32)
    both = jnp.stack((gate_part, up_part), axis=0)
    summed = lax.psum_scatter(both, "dp", scatter_dimension=2, tiled=True)
    hidden = (jax.nn.silu(summed[0]) * summed[1]).astype(jnp.bfloat16)
    hidden = lax.all_gather(hidden, "dp", axis=1, tiled=True)
    result = jnp.einsum("emf,edf->emd", hidden, w_down, preferred_element_type=jnp.float32)
    result = result.astype(jnp.bfloat16).reshape(held_count, blk_size, capacity, width_dev)
    high = weighted.astype(jnp.bfloat16)
    low = (weighted - high.astype(jnp.float32)).astype(jnp.bfloat16)
    partial = jnp.einsum(
        "bhpt,hbpd->btd", high, result, preferred_element_type=jnp.float32
    ) + jnp.einsum("bhpt,hbpd->btd", low, result, preferred_element_type=jnp.float32)
    partial = partial.astype(jnp.bfloat16).reshape(blk_size * tok_rows, width_dev)
    return lax.psum_scatter(partial, "blk", scatter_dimension=0, tiled=True)


def choose(tokens, expert_ids, gate_vals, w_gate, w_up, w_down):
    n_blk, held = lax.axis_size("blk"), w_gate.shape[0]
    capacity = 2 * tokens.shape[0] * expert_ids.shape[1] // (held * n_blk)
    fits = lax.axis_size("dp") == 4 and held == 2 and n_blk == 8 and capacity % 32 == 0
    fits = fits and w_gate.shape[2] % (2 * TILE) == 0 and tokens.shape[1] % DOWN == 0
    body = fused if fits else local
    return body(tokens, expert_ids, gate_vals, w_gate, w_up, w_down)


def solution(mesh):
    return jax.shard_map(
        choose,
        mesh=mesh,
        in_specs=(
            P("blk", "dp"),
            P("blk", None),
            P("blk", None),
            P("blk", "dp", None),
            P("blk", "dp", None),
            P("blk", "dp", None),
        ),
        out_specs=P("blk", "dp"),
        check_vma=False,
    )
```

time: 130 us -> 120 us (0.923)
  Pallas kernels: 126 us -> 116 us
    pallas_call x1, Pallas kernels: 126 us -> 116 us  [fused(): pl.pallas_call(functools.partial(fused_kernel, n_blk), out_shape=jax.Shap...]
where the time goes in v1:
time: 120 us
  Pallas kernels  116 us (97%)
  other arithmetic  1.98 us (2%)
  local copies, waits for them, and re-layouts  1.72 us (1%)
    pallas_call x1, Pallas kernels, fused(): pl.pallas_call(functools.partial(fused_kernel, n_blk), out_shape=jax.Shap...  116 us

profile of v1, /device:TPU:0, one launch (start us, length us, event | category | flops | bytes accessed | tf_op | source)
XLA Modules:
  0.0 120.1 jit_solution(9113831994466606114)
XLA Ops:
  0.0 0.7 convert_bitcast_fusion
  0.7 1.3 %select_maximum_fusion.info_ref = f32[16,128]{1,0:T(8,128)} fusion(f32[6,128]{1,0:T(8,128)} %bitcast.3, f32[6,128]{1,0:T(8,128)S(1)} %convert_bitcast_fusion), kind=kLoop, calls=%fused_computation | loop fusion | flops 10240 | bytes 14336 | tf_op jit(solution)/shard_map/concatenate | solution.py:299
  2.0 116.4 %shard_map.64 = bf16[128,1280]{1,0:T(8,128)(2,1)} custom-call(bf16[128,1280]{1,0:T(8,128)(2,1)} %tok_ref.1, f32[16,128]{1,0:T(8,128)} %select_maximum_fusion.info_ref, bf16[2,1280,1536]{2,1,0:T(8,128)(2,1)} %wg_hbm.1, bf16[2,1280,1536]{2,1,0:T(8,128)(2,1)} %wu_hbm.1, bf16[2,1280,1536]{2,1,0:T(8,128)(2,1)} %wd_hbm.1), custom_call_target="tpu_custom_call" | custom-call | tf_op jit(solution)/shard_map/pallas_call | solution.py:305
  118.4 1.7 %copy.8 = bf16[128,1280]{1,0:T(8,128)(2,1)} copy(bf16[128,1280]{1,0:T(8,128)(2,1)} %shard_map.64) | data formatting | bytes 655360

commit v2 on v1

--- a/solution.py
+++ b/solution.py
@@ -11,6 +11,7 @@
 VMEM_BYTES = 66_000_000
 TILE = 384
 DOWN = 256
+ORDER = (0, 2, 4, 5, 7, 6, 1, 3)
 
 
 def flip(a, m, size):
@@ -22,7 +23,7 @@
 
 
 def fused_kernel(
-    n_blk, tok_ref, info_ref, wg_hbm, wu_hbm, wd_hbm, out_ref,
+    n_blk, tok_ref, ids_ref, gates_ref, wg_hbm, wu_hbm, wd_hbm, out_ref,
     wg, wu, wd, everyone, routed, part, near, far_out, far_in, hidden, rows_out,
     outgoing, arrived, hold, acc, info, high, low, hot,
     w_sem, tok_s, tok_r, near_s, near_r, far_s, far_r, hy_s, hy_r, hc_s, hc_r, hf_s, hf_r, ret_s, ret_r, info_s, info_r,
@@ -48,17 +49,27 @@
         return (flip(blk, m, n_blk), dp)
 
     def mask_of(i):
-        m = jnp.where(i == 0, 0, jnp.where(i == 1, 2, i + 2))
-        return jnp.where(i == n_blk - 2, 3, jnp.where(i == n_blk - 1, 1, m))
+        m = 0
+        for k in range(1, n_blk):
+            m = jnp.where(i == k, ORDER[k], m)
+        return m
 
     def tok_direct(m):
         return copy(tok_ref, everyone.at[m], tok_s.at[m], tok_r.at[m], peer(m))
 
     def info_direct(m):
-        return copy(info_ref, info.at[m], info_s.at[m], info_r.at[m], peer(m))
+        return copy(info.at[0], info.at[m], info_s.at[m], info_r.at[m], peer(m))
+
+    def tok_relay(have, m, k, to):
+        return copy(everyone.at[have], everyone.at[m], tok_s.at[k], tok_r.at[m], peer(to))
 
     def tok_onward(m):
-        return copy(everyone.at[m], everyone.at[m + 1], tok_s.at[m + 1], tok_r.at[m + 1], peer(1))
+        return tok_relay(m, m + 1, m + 1, 1)
+
+    def tok_middle():
+        return copy(tok_ref, everyone.at[6], tok_s.at[0], tok_r.at[6], peer(6))
+
+    relays = ((2, 4, 4, 6), (6, 4, 6, 2), (4, 6, n_blk, 2))
 
     def near_copy(u):
         return copy(part.at[0], near.at[u], near_s.at[u], near_r.at[u], mate)
@@ -76,7 +87,7 @@
         return copy(hidden.at[u, c, 1 - y], hidden.at[u, c, 1 - y], hf_s.at[u], hf_r.at[u], mate)
 
     def ret_copy(m):
-        to = jnp.where(lax.rem(m, 2) == 1, 1, m)
+        to = jnp.where((lax.rem(m, 2) == 1) & (m > 3), 1, m)
         return copy(outgoing.at[m], arrived.at[m], ret_s.at[m], ret_r.at[m], peer(to))
 
     def load(k, h):
@@ -85,6 +96,14 @@
 
     load(0, 0).start()
     load(1, 0).start()
+
+    tok_rows = tok_ref.shape[0]
+    top_k = ids_ref.shape[0]
+    lines = info.shape[1] // 2
+    inner = lax.rem(lax.div(lax.div(blk, 2) + 1, 2), 2) == 1
+    info[0] = jnp.full(info.shape[1:], -1.0, jnp.float32)
+    info[0, :top_k] = ids_ref[...].astype(jnp.float32)
+    info[0, lines:lines + top_k] = gates_ref[...]
 
     barrier = pltpu.get_barrier_semaphore()
     for m in range(1, n_blk):
@@ -95,12 +114,14 @@
 
     for m in range(1, n_blk):
         info_direct(m).start()
-    for m in [1] + list(range(2, n_blk - 2, 2)):
+    for m in (1, 2):
         tok_direct(m).start()
+
+    @pl.when(inner)
+    def _():
+        tok_middle().start()
+
     everyone[0] = tok_ref[...]
-    info[0] = info_ref[...]
-    tok_rows = tok_ref.shape[0]
-    lines = info_ref.shape[0] // 2
 
     def slots_of(m):
         square = (tok_rows, tok_rows)
@@ -132,13 +153,35 @@
             def _():
                 info_direct(m).wait_recv()
 
-                @pl.when((lax.rem(m, 2) == 1) | (m == 2))
+                @pl.when(m != 6)
                 def _():
                     tok_direct(m).wait_recv()
 
                 @pl.when(m == 2)
                 def _():
-                    tok_onward(m).start()
+                    @pl.when(inner)
+                    def _():
+                        tok_relay(*relays[0]).start()
+                        tok_direct(6).wait_recv()
+                        tok_relay(*relays[1]).start()
+
+                    tok_onward(2).start()
+
+                @pl.when(m == 4)
+                def _():
+                    @pl.when(inner)
+                    def _():
+                        tok_relay(*relays[2]).start()
+
+                    tok_onward(4).start()
+
+                @pl.when(m == 5)
+                def _():
+                    @pl.when(jnp.logical_not(inner))
+                    def _():
+                        tok_direct(6).wait_recv()
+
+                    tok_onward(6).start()
 
             slots_of(m)
 
@@ -223,38 +266,38 @@
             def _():
                 acc[...] = mixed
 
-            @pl.when((m > 0) & (lax.rem(m, 2) == 0))
-            def _():
-                hold[lax.div(m, 2) - 1] = mixed
-
-            @pl.when(lax.rem(m, 2) == 1)
+            @pl.when((m > 2) & (lax.rem(m, 2) == 0))
+            def _():
+                hold[lax.div(m, 2) - 2] = mixed
+
+            @pl.when((lax.rem(m, 2) == 1) | (m == 2))
             def _():
                 outgoing[m] = mixed.astype(jnp.bfloat16)
                 ret_copy(m).start()
 
-    def spread(u):
-        @pl.when(u == 3)
-        def _():
-            tok_direct(n_blk - 2).start()
-
-        m = mask_of(jnp.minimum(lax.div(u + 1, held), n_blk - 1))
-
-        @pl.when((lax.rem(u, held) == held - 1) & (m > 2) & (lax.rem(m, 2) == 0))
-        def _():
-            tok_direct(m).wait_recv()
-            tok_onward(m).start()
-
     def merge(u):
-        i = lax.div(u, held)
-        m = mask_of(jnp.maximum(i - 1, 0)) - 1
-
-        @pl.when((lax.rem(u, held) == held - 1) & (m > 0) & (lax.rem(m, 2) == 0))
+        m = jnp.where(u == 9, 4, 6)
+
+        @pl.when((u == 9) | (u == 11))
         def _():
             ret_copy(m + 1).wait_recv()
-            outgoing[m] = (hold[lax.div(m, 2) - 1] + arrived[m + 1].astype(jnp.float32)).astype(jnp.bfloat16)
+            total = hold[lax.div(m, 2) - 2] + arrived[m + 1].astype(jnp.float32)
+            outgoing[m] = total.astype(jnp.bfloat16)
             ret_copy(m).start()
 
-    stages = ((1, join), (0, project), (2, activate), (3, relay), (4, finish), (0, spread), (4, merge))
+    def early(u):
+        @pl.when(u == units - 3)
+        def _():
+            finish(u)
+
+    def late(u):
+        @pl.when(u != units - 3)
+        def _():
+            finish(u)
+
+    stages = (
+        (1, join), (4, early), (2, activate), (0, project), (3, relay), (4, late), (4, merge),
+    )
 
     def step(s, carry):
         for lag, stage in stages:
@@ -265,10 +308,15 @@
 
     lax.fori_loop(0, units + 4, step, 0)
 
-    for m in [4, 6, 1, 2]:
-        ret_copy(m).wait_recv()
-        acc[...] += arrived[m].astype(jnp.float32)
-    out_ref[...] = acc[...].astype(jnp.bfloat16)
+    def gathered(total, masks):
+        for m in masks:
+            ret_copy(m).wait_recv()
+        for m in masks:
+            total = total + arrived[m].astype(jnp.float32)
+        return total
+
+    acc[...] = gathered(acc[...], range(2, n_blk, 2))
+    out_ref[...] = gathered(acc[...], (1, 3)).astype(jnp.bfloat16)
 
     def drain(u, carry):
         far_copy(u).wait_send()
@@ -279,9 +327,19 @@
 
     def drain_blocks(m, carry):
         info_direct(m).wait_send()
-        tok_direct(m).wait_send()
         ret_copy(m).wait_send()
         return carry
+
+    for m in (1, 2):
+        tok_direct(m).wait_send()
+    for m in (2, 4, 6):
+        tok_onward(m).wait_send()
+
+    @pl.when(inner)
+    def _():
+        tok_middle().wait_send()
+        for hop in relays:
+            tok_relay(*hop).wait_send()
 
     lax.fori_loop(0, units, drain, 0)
     lax.fori_loop(1, n_blk, drain_blocks, 0)
@@ -294,18 +352,16 @@
     capacity = 2 * tok_rows * expert_ids.shape[1] // (held * n_blk)
     half, units = capacity // 2, held * n_blk
     top_k = expert_ids.shape[1]
-    spare = ((0, -top_k % 8), (0, 0))
-    ids = jnp.pad(expert_ids.T.astype(jnp.float32), spare, constant_values=-1.0)
-    packed = jnp.concatenate((ids, jnp.pad(gate_vals.T, spare)), axis=0)
+    lines = top_k + -top_k % 8
     bf, f32 = jnp.bfloat16, jnp.float32
     dma = pltpu.SemaphoreType.DMA
-    counts = [n_blk] * 2 + [units] * 10 + [n_blk] * 4
+    counts = [n_blk + 1, n_blk] + [units] * 10 + [n_blk] * 4
     vmem = pl.BlockSpec(memory_space=pltpu.VMEM)
     anywhere = pl.BlockSpec(memory_space=pl.ANY)
     return pl.pallas_call(
         functools.partial(fused_kernel, n_blk),
         out_shape=jax.ShapeDtypeStruct((tok_rows, width), bf),
-        in_specs=[vmem] * 2 + [anywhere] * 3,
+        in_specs=[vmem] * 3 + [anywhere] * 3,
         out_specs=vmem,
         scratch_shapes=[
             pltpu.VMEM(w_gate.shape, bf),
@@ -321,9 +377,9 @@
             pltpu.VMEM((held, capacity, width), bf),
             pltpu.VMEM((n_blk, tok_rows, width), bf),
             pltpu.VMEM((n_blk, tok_rows, width), bf),
-            pltpu.VMEM((n_blk // 2 - 1, tok_rows, width), f32),
+            pltpu.VMEM((n_blk // 2 - 2, tok_rows, width), f32),
             pltpu.VMEM((tok_rows, width), f32),
-            pltpu.VMEM((n_blk,) + packed.shape, f32),
+            pltpu.VMEM((n_blk, 2 * lines, tok_rows), f32),
             pltpu.VMEM((n_blk, held * capacity, tok_rows), bf),
             pltpu.VMEM((n_blk, held * capacity, tok_rows), bf),
             pltpu.VMEM((held, capacity, tok_rows), bf),
@@ -332,7 +388,7 @@
         compiler_params=pltpu.CompilerParams(
             collective_id=0, has_side_effects=True, vmem_limit_bytes=VMEM_BYTES
         ),
-    )(tokens, packed, w_gate, w_up, w_down)
+    )(tokens, expert_ids.T, gate_vals.T, w_gate, w_up, w_down)
 
 
 def routing(expert_ids, gate_vals, held_count, capacity):

time: 120 us -> 107 us (0.89)
  Pallas kernels: 116 us -> 105 us
  other arithmetic: 1.98 us -> 0 us
    pallas_call x1, Pallas kernels: 116 us -> 105 us  [fused(): pl.pallas_call(functools.partial(fused_kernel, n_blk), out_shape=jax.Shap...]
    concatenate x1 -> x0, other arithmetic: 1.29 us -> none  [fused(): packed = jnp.concatenate((ids, jnp.pad(gate_vals.T, spare)), axis=0)]
where the time goes in v2:
time: 107 us
  Pallas kernels  105 us (98%)
  local copies, waits for them, and re-layouts  1.72 us (2%)
    pallas_call x1, Pallas kernels, fused(): pl.pallas_call(functools.partial(fused_kernel, n_blk), out_shape=jax.Shap...  105 us

profile of v2, /device:TPU:0, one launch (start us, length us, event | category | flops | bytes accessed | tf_op | source)
XLA Modules:
  0.0 107.1 jit_solution(13594956902140105908)
XLA Ops:
  0.0 105.3 %shard_map.64 = bf16[128,1280]{1,0:T(8,128)(2,1)} custom-call(bf16[128,1280]{1,0:T(8,128)(2,1)} %tok_ref.1, s32[6,128]{1,0:T(8,128)} %bitcast.2, f32[6,128]{1,0:T(8,128)} %bitcast.3, bf16[2,1280,1536]{2,1,0:T(8,128)(2,1)} %wg_hbm.1, bf16[2,1280,1536]{2,1,0:T(8,128)(2,1)} %wu_hbm.1, bf16[2,1280,1536]{2,1,0:T(8,128)(2,1)} %wd_hbm.1), custom_call_target="tpu_custom_call" | custom-call | tf_op jit(solution)/shard_map/pallas_call | solution.py:361
  105.4 1.7 %copy.8 = bf16[128,1280]{1,0:T(8,128)(2,1)} copy(bf16[128,1280]{1,0:T(8,128)(2,1)} %shard_map.64) | data formatting | bytes 655360

commit v3 on v2

--- a/solution.py
+++ b/solution.py
@@ -11,6 +11,7 @@
 VMEM_BYTES = 66_000_000
 TILE = 384
 DOWN = 256
+RING = 4
 ORDER = (0, 2, 4, 5, 7, 6, 1, 3)
 
 
@@ -71,20 +72,23 @@
 
     relays = ((2, 4, 4, 6), (6, 4, 6, 2), (4, 6, n_blk, 2))
 
-    def near_copy(u):
-        return copy(part.at[0], near.at[u], near_s.at[u], near_r.at[u], mate)
+    def near_copy(u, which):
+        k, span = lax.rem(u, 2), slice(which * cols, (which + 1) * cols)
+        return copy(
+            part.at[0, :, :, span], near.at[u, :, :, span], near_s.at[k, which], near_r.at[k, which], mate
+        )
 
     def far_copy(u):
-        return copy(far_out.at[u], far_in.at[u], far_s.at[u], far_r.at[u], across)
+        return copy(far_out.at[u], far_in.at[u], far_s.at[lax.rem(u, RING)], far_r.at[lax.rem(u, RING)], across)
 
     def hidden_far(u):
-        return copy(hidden.at[u, c, y], hidden.at[u, c, y], hy_s.at[u], hy_r.at[u], across)
+        return copy(hidden.at[u, c, y], hidden.at[u, c, y], hy_s.at[lax.rem(u, RING)], hy_r.at[lax.rem(u, RING)], across)
 
     def hidden_near(u):
-        return copy(hidden.at[u, c, y], hidden.at[u, c, y], hc_s.at[u], hc_r.at[u], mate)
+        return copy(hidden.at[u, c, y], hidden.at[u, c, y], hc_s.at[lax.rem(u, RING)], hc_r.at[lax.rem(u, RING)], mate)
 
     def hidden_onward(u):
-        return copy(hidden.at[u, c, 1 - y], hidden.at[u, c, 1 - y], hf_s.at[u], hf_r.at[u], mate)
+        return copy(hidden.at[u, c, 1 - y], hidden.at[u, c, 1 - y], hf_s.at[lax.rem(u, RING)], hf_r.at[lax.rem(u, RING)], mate)
 
     def ret_copy(m):
         to = jnp.where((lax.rem(m, 2) == 1) & (m > 3), 1, m)
@@ -94,8 +98,17 @@
         hbm, vmem = ((wg_hbm, wg), (wu_hbm, wu), (wd_hbm, wd))[k]
         return pltpu.make_async_copy(hbm.at[h], vmem.at[h], w_sem.at[k, h])
 
-    load(0, 0).start()
-    load(1, 0).start()
+    def columns(side):
+        return pl.multiple_of(jnp.where(c == side, cols, 0), 128)
+
+    def load_side(k, side):
+        hbm, vmem = ((wg_hbm, wg), (wu_hbm, wu))[k]
+        span = (0, slice(None), pl.ds(columns(side), cols))
+        return pltpu.make_async_copy(hbm.at[span], vmem.at[span], w_sem.at[3 + k, side])
+
+    for side in range(2):
+        for k in range(2):
+            load_side(k, side).start()
 
     tok_rows = tok_ref.shape[0]
     top_k = ids_ref.shape[0]
@@ -112,14 +125,15 @@
         pl.semaphore_signal(barrier, inc=1, device_id=device, device_id_type=MESH)
     pl.semaphore_wait(barrier, n_blk + 1)
 
-    for m in range(1, n_blk):
-        info_direct(m).start()
-    for m in (1, 2):
+    for m in (2, 1):
         tok_direct(m).start()
 
     @pl.when(inner)
     def _():
         tok_middle().start()
+
+    for m in range(1, n_blk):
+        info_direct(m).start()
 
     everyone[0] = tok_ref[...]
 
@@ -189,22 +203,22 @@
             hot[h], everyone[m], preferred_element_type=jnp.float32
         ).astype(jnp.bfloat16)
 
-        @pl.when(i == 0)
-        def _():
-            load(0, h).wait()
-            load(1, h).wait()
-
-            @pl.when(h == 0)
-            def _():
-                load(0, 1).start()
-                load(1, 1).start()
-
-            @pl.when(h == 1)
-            def _():
-                load(2, 0).start()
-                load(2, 1).start()
+        @pl.when(u == 1)
+        def _():
+            load(0, 1).wait()
+            load(1, 1).wait()
+            load(2, 0).start()
+            load(2, 1).start()
 
         for side in range(2):
+            @pl.when(u == 0)
+            def _():
+                load_side(0, side).wait()
+                load_side(1, side).wait()
+                if side == 1:
+                    load(0, 1).start()
+                    load(1, 1).start()
+
             first = jnp.where(c == side, cols, 0)
             for which, w in enumerate((wg, wu)):
                 for f in range(0, cols, TILE):
@@ -215,17 +229,18 @@
                     span = slice(which * cols + f, which * cols + f + TILE)
                     part[side, 0, :, span] = got[:half]
                     part[side, 1, :, span] = got[half:]
-            if side == 0:
-                near_copy(u).start()
+                if side == 0:
+                    near_copy(u, which).start()
 
     def join(u):
-        near_copy(u).wait()
+        near_copy(u, 0).wait()
+        near_copy(u, 1).wait()
         far_out[u] = (part[1, 1 - y] + near[u, 1 - y]).astype(jnp.bfloat16)
         far_copy(u).start()
         near[u, y] = near[u, y] + part[1, y]
 
     def activate(u):
-        far_copy(u).wait_recv()
+        far_copy(u).wait()
         gate = near[u, y, :, :cols] + far_in[u, :, :cols].astype(jnp.float32)
         up = near[u, y, :, cols:] + far_in[u, :, cols:].astype(jnp.float32)
         hidden[u, c, y] = (gate / (1.0 + jnp.exp(-gate)) * up).astype(jnp.bfloat16)
@@ -233,7 +248,7 @@
         hidden_near(u).start()
 
     def relay(u):
-        hidden_far(u).wait_recv()
+        hidden_far(u).wait()
         hidden_onward(u).start()
 
     def finish(u):
@@ -244,8 +259,8 @@
         def _():
             load(2, h).wait()
 
-        hidden_near(u).wait_recv()
-        hidden_onward(u).wait_recv()
+        hidden_near(u).wait()
+        hidden_onward(u).wait()
         rows = jnp.concatenate([hidden[u, k].reshape(cap, cols) for k in range(2)], axis=1)
         for d in range(0, width, DOWN):
             rows_out[h, :, d:d + DOWN] = lax.dot_general(
@@ -308,28 +323,11 @@
 
     lax.fori_loop(0, units + 4, step, 0)
 
-    def gathered(total, masks):
-        for m in masks:
-            ret_copy(m).wait_recv()
-        for m in masks:
-            total = total + arrived[m].astype(jnp.float32)
-        return total
-
-    acc[...] = gathered(acc[...], range(2, n_blk, 2))
-    out_ref[...] = gathered(acc[...], (1, 3)).astype(jnp.bfloat16)
-
-    def drain(u, carry):
-        far_copy(u).wait_send()
-        hidden_far(u).wait_send()
-        hidden_near(u).wait_send()
-        hidden_onward(u).wait_send()
+    def drain(m, carry):
+        info_direct(m).wait_send()
         return carry
 
-    def drain_blocks(m, carry):
-        info_direct(m).wait_send()
-        ret_copy(m).wait_send()
-        return carry
-
+    lax.fori_loop(1, n_blk, drain, 0)
     for m in (1, 2):
         tok_direct(m).wait_send()
     for m in (2, 4, 6):
@@ -341,8 +339,17 @@
         for hop in relays:
             tok_relay(*hop).wait_send()
 
-    lax.fori_loop(0, units, drain, 0)
-    lax.fori_loop(1, n_blk, drain_blocks, 0)
+    for m in (2, 4, 6):
+        ret_copy(m).wait_recv()
+    acc[...] = acc[...] + sum(arrived[m].astype(jnp.float32) for m in (2, 4, 6))
+    for m in (1, 2, 4, 5, 6, 7):
+        ret_copy(m).wait_send()
+    for m in (1, 3):
+        ret_copy(m).wait_recv()
+    out_ref[...] = (
+        acc[...] + arrived[1].astype(jnp.float32) + arrived[3].astype(jnp.float32)
+    ).astype(jnp.bfloat16)
+    ret_copy(3).wait_send()
 
 
 def fused(tokens, expert_ids, gate_vals, w_gate, w_up, w_down):
@@ -355,12 +362,12 @@
     lines = top_k + -top_k % 8
     bf, f32 = jnp.bfloat16, jnp.float32
     dma = pltpu.SemaphoreType.DMA
-    counts = [n_blk + 1, n_blk] + [units] * 10 + [n_blk] * 4
+    counts = [n_blk + 1, n_blk, (2, 2), (2, 2)] + [RING] * 8 + [n_blk] * 4
     vmem = pl.BlockSpec(memory_space=pltpu.VMEM)
     anywhere = pl.BlockSpec(memory_space=pl.ANY)
     return pl.pallas_call(
         functools.partial(fused_kernel, n_blk),
-        out_shape=jax.ShapeDtypeStruct((tok_rows, width), bf),
+        out_shape=pltpu.VMEM((tok_rows, width), bf),
         in_specs=[vmem] * 3 + [anywhere] * 3,
         out_specs=vmem,
         scratch_shapes=[
@@ -383,8 +390,8 @@
             pltpu.VMEM((n_blk, held * capacity, tok_rows), bf),
             pltpu.VMEM((n_blk, held * capacity, tok_rows), bf),
             pltpu.VMEM((held, capacity, tok_rows), bf),
-            dma((3, held)),
-        ] + [dma((count,)) for count in counts],
+            dma((5, 2)),
+        ] + [dma(count if isinstance(count, tuple) else (count,)) for count in counts],
         compiler_params=pltpu.CompilerParams(
             collective_id=0, has_side_effects=True, vmem_limit_bytes=VMEM_BYTES
         ),

time: 107 us -> 104 us (0.972)
  Pallas kernels: 105 us -> 103 us
    pallas_call x1, Pallas kernels: 105 us -> 103 us  [fused(): pl.pallas_call(functools.partial(fused_kernel, n_blk), out_shape=pltpu.VM...]
where the time goes in v3:
time: 104 us
  Pallas kernels  103 us (99%)
    pallas_call x1, Pallas kernels, fused(): pl.pallas_call(functools.partial(fused_kernel, n_blk), out_shape=pltpu.VM...  103 us

profile of v3, /device:TPU:0, one launch (start us, length us, event | category | flops | bytes accessed | tf_op | source)
XLA Modules:
  0.0 103.6 jit_solution(508907422502841359)
XLA Ops:
  0.0 102.8 %shard_map.64 = bf16[128,1280]{1,0:T(8,128)(2,1)S(1)} custom-call(bf16[128,1280]{1,0:T(8,128)(2,1)} %tok_ref.1, s32[6,128]{1,0:T(8,128)} %bitcast.2, f32[6,128]{1,0:T(8,128)} %bitcast.3, bf16[2,1280,1536]{2,1,0:T(8,128)(2,1)} %wg_hbm.1, bf16[2,1280,1536]{2,1,0:T(8,128)(2,1)} %wu_hbm.1, bf16[2,1280,1536]{2,1,0:T(8,128)(2,1)} %wd_hbm.1), custom_call_target="tpu_custom_call" | custom-call | tf_op jit(solution)/shard_map/pallas_call | solution.py:368
  102.9 0.7 copy.8

commit v4 on v3

--- a/solution.py
+++ b/solution.py
@@ -55,20 +55,36 @@
             m = jnp.where(i == k, ORDER[k], m)
         return m
 
-    def tok_direct(m):
-        return copy(tok_ref, everyone.at[m], tok_s.at[m], tok_r.at[m], peer(m))
-
-    def info_direct(m):
-        return copy(info.at[0], info.at[m], info_s.at[m], info_r.at[m], peer(m))
-
-    def tok_relay(have, m, k, to):
-        return copy(everyone.at[have], everyone.at[m], tok_s.at[k], tok_r.at[m], peer(to))
-
-    def tok_onward(m):
-        return tok_relay(m, m + 1, m + 1, 1)
-
-    def tok_middle():
-        return copy(tok_ref, everyone.at[6], tok_s.at[0], tok_r.at[6], peer(6))
+    def hop(m, k, to, have):
+        tok, ids = (tok_ref, info.at[0]) if have is None else (everyone.at[have], info.at[have])
+        return (
+            copy(tok, everyone.at[m], tok_s.at[k], tok_r.at[m], peer(to)),
+            copy(ids, info.at[m], info_s.at[k], info_r.at[m], peer(to)),
+        )
+
+    def send(hops):
+        for part_of in hops:
+            part_of.start()
+
+    def sent(hops):
+        for part_of in hops:
+            part_of.wait_send()
+
+    def received(m):
+        for part_of in hop(m, m, m, None):
+            part_of.wait_recv()
+
+    def direct(m):
+        return hop(m, m, m, None)
+
+    def relay_hop(have, m, k, to):
+        return hop(m, k, to, have)
+
+    def onward(m):
+        return hop(m + 1, m + 1, 1, m)
+
+    def middle():
+        return hop(6, 0, 6, None)
 
     relays = ((2, 4, 4, 6), (6, 4, 6, 2), (4, 6, n_blk, 2))
 
@@ -119,21 +135,21 @@
     info[0, lines:lines + top_k] = gates_ref[...]
 
     barrier = pltpu.get_barrier_semaphore()
-    for m in range(1, n_blk):
-        pl.semaphore_signal(barrier, inc=1, device_id=peer(m), device_id_type=MESH)
-    for device in (mate, across):
+    for device in (peer(2), peer(1), mate, across):
         pl.semaphore_signal(barrier, inc=1, device_id=device, device_id_type=MESH)
-    pl.semaphore_wait(barrier, n_blk + 1)
-
-    for m in (2, 1):
-        tok_direct(m).start()
 
     @pl.when(inner)
     def _():
-        tok_middle().start()
-
-    for m in range(1, n_blk):
-        info_direct(m).start()
+        pl.semaphore_signal(barrier, inc=1, device_id=peer(6), device_id_type=MESH)
+
+    pl.semaphore_wait(barrier, 4 + jnp.where(inner, 1, 0))
+
+    send(direct(2))
+    send(direct(1))
+
+    @pl.when(inner)
+    def _():
+        send(middle())
 
     everyone[0] = tok_ref[...]
 
@@ -165,37 +181,35 @@
         def _():
             @pl.when(i > 0)
             def _():
-                info_direct(m).wait_recv()
-
                 @pl.when(m != 6)
                 def _():
-                    tok_direct(m).wait_recv()
+                    received(m)
 
                 @pl.when(m == 2)
                 def _():
                     @pl.when(inner)
                     def _():
-                        tok_relay(*relays[0]).start()
-                        tok_direct(6).wait_recv()
-                        tok_relay(*relays[1]).start()
-
-                    tok_onward(2).start()
+                        send(relay_hop(*relays[0]))
+                        received(6)
+                        send(relay_hop(*relays[1]))
+
+                    send(onward(2))
 
                 @pl.when(m == 4)
                 def _():
                     @pl.when(inner)
                     def _():
-                        tok_relay(*relays[2]).start()
-
-                    tok_onward(4).start()
+                        send(relay_hop(*relays[2]))
+
+                    send(onward(4))
 
                 @pl.when(m == 5)
                 def _():
                     @pl.when(jnp.logical_not(inner))
                     def _():
-                        tok_direct(6).wait_recv()
-
-                    tok_onward(6).start()
+                        received(6)
+
+                    send(onward(6))
 
             slots_of(m)
 
@@ -215,7 +229,7 @@
             def _():
                 load_side(0, side).wait()
                 load_side(1, side).wait()
-                if side == 1:
+                if side == 0:
                     load(0, 1).start()
                     load(1, 1).start()
 
@@ -323,21 +337,16 @@
 
     lax.fori_loop(0, units + 4, step, 0)
 
-    def drain(m, carry):
-        info_direct(m).wait_send()
-        return carry
-
-    lax.fori_loop(1, n_blk, drain, 0)
     for m in (1, 2):
-        tok_direct(m).wait_send()
+        sent(direct(m))
     for m in (2, 4, 6):
-        tok_onward(m).wait_send()
+        sent(onward(m))
 
     @pl.when(inner)
     def _():
-        tok_middle().wait_send()
-        for hop in relays:
-            tok_relay(*hop).wait_send()
+        sent(middle())
+        for args in relays:
+            sent(relay_hop(*args))
 
     for m in (2, 4, 6):
         ret_copy(m).wait_recv()
@@ -362,7 +371,7 @@
     lines = top_k + -top_k % 8
     bf, f32 = jnp.bfloat16, jnp.float32
     dma = pltpu.SemaphoreType.DMA
-    counts = [n_blk + 1, n_blk, (2, 2), (2, 2)] + [RING] * 8 + [n_blk] * 4
+    counts = [n_blk + 1, n_blk, (2, 2), (2, 2)] + [RING] * 8 + [n_blk] * 2 + [n_blk + 1, n_blk]
     vmem = pl.BlockSpec(memory_space=pltpu.VMEM)
     anywhere = pl.BlockSpec(memory_space=pl.ANY)
     return pl.pallas_call(

time: 104 us -> 102 us (0.981)
    pallas_call x1, Pallas kernels: 103 us -> 102 us  [fused(): pl.pallas_call(functools.partial(fused_kernel, n_blk), out_shape=pltpu.VM...]
where the time goes in v4:
time: 102 us
  Pallas kernels  102 us (100%)
    pallas_call x1, Pallas kernels, fused(): pl.pallas_call(functools.partial(fused_kernel, n_blk), out_shape=pltpu.VM...  102 us

profile of v4, /device:TPU:0, one launch (start us, length us, event | category | flops | bytes accessed | tf_op | source)
XLA Modules:
  0.0 102.2 jit_solution(8829859016565400124)
XLA Ops:
  0.0 101.5 %shard_map.64 = bf16[128,1280]{1,0:T(8,128)(2,1)S(1)} custom-call(bf16[128,1280]{1,0:T(8,128)(2,1)} %tok_ref.1, s32[6,128]{1,0:T(8,128)} %bitcast.2, f32[6,128]{1,0:T(8,128)} %bitcast.3, bf16[2,1280,1536]{2,1,0:T(8,128)(2,1)} %wg_hbm.1, bf16[2,1280,1536]{2,1,0:T(8,128)(2,1)} %wu_hbm.1, bf16[2,1280,1536]{2,1,0:T(8,128)(2,1)} %wd_hbm.1), custom_call_target="tpu_custom_call" | custom-call | tf_op jit(solution)/shard_map/pallas_call | solution.py:377
  101.5 0.7 copy.8

commit v5 on v4

--- a/solution.py
+++ b/solution.py
@@ -24,9 +24,9 @@
 
 
 def fused_kernel(
-    n_blk, tok_ref, ids_ref, gates_ref, wg_hbm, wu_hbm, wd_hbm, out_ref,
+    n_blk, tok_hbm, ids_hbm, gates_hbm, wg_hbm, wu_hbm, wd_hbm, out_ref,
     wg, wu, wd, everyone, routed, part, near, far_out, far_in, hidden, rows_out,
-    outgoing, arrived, hold, acc, info, high, low, hot,
+    outgoing, arrived, hold, acc, ids_ref, gates_ref, info, high, low, hot,
     w_sem, tok_s, tok_r, near_s, near_r, far_s, far_r, hy_s, hy_r, hc_s, hc_r, hf_s, hf_r, ret_s, ret_r, info_s, info_r,
 ):
     blk = lax.axis_index("blk")
@@ -56,7 +56,7 @@
         return m
 
     def hop(m, k, to, have):
-        tok, ids = (tok_ref, info.at[0]) if have is None else (everyone.at[have], info.at[have])
+        tok, ids = (everyone.at[have or 0], info.at[have or 0])
         return (
             copy(tok, everyone.at[m], tok_s.at[k], tok_r.at[m], peer(to)),
             copy(ids, info.at[m], info_s.at[k], info_r.at[m], peer(to)),
@@ -94,8 +94,11 @@
             part.at[0, :, :, span], near.at[u, :, :, span], near_s.at[k, which], near_r.at[k, which], mate
         )
 
-    def far_copy(u):
-        return copy(far_out.at[u], far_in.at[u], far_s.at[lax.rem(u, RING)], far_r.at[lax.rem(u, RING)], across)
+    def far_copy(u, which):
+        k, span = lax.rem(u, RING), slice(which * cols, (which + 1) * cols)
+        return copy(
+            far_out.at[u, :, span], far_in.at[u, :, span], far_s.at[k, which], far_r.at[k, which], across
+        )
 
     def hidden_far(u):
         return copy(hidden.at[u, c, y], hidden.at[u, c, y], hy_s.at[lax.rem(u, RING)], hy_r.at[lax.rem(u, RING)], across)
@@ -122,26 +125,34 @@
         span = (0, slice(None), pl.ds(columns(side), cols))
         return pltpu.make_async_copy(hbm.at[span], vmem.at[span], w_sem.at[3 + k, side])
 
+    inputs = [
+        pltpu.make_async_copy(ids_hbm, ids_ref, w_sem.at[5, 0]),
+        pltpu.make_async_copy(gates_hbm, gates_ref, w_sem.at[5, 1]),
+        pltpu.make_async_copy(tok_hbm, everyone.at[0], w_sem.at[2, 0]),
+    ]
+    for load_in in inputs:
+        load_in.start()
     for side in range(2):
         for k in range(2):
             load_side(k, side).start()
 
-    tok_rows = tok_ref.shape[0]
+    inner = lax.rem(lax.div(lax.div(blk, 2) + 1, 2), 2) == 1
+    barrier = pltpu.get_barrier_semaphore()
+    for device in (peer(2), peer(1), mate, across):
+        pl.semaphore_signal(barrier, inc=1, device_id=device, device_id_type=MESH)
+
+    @pl.when(inner)
+    def _():
+        pl.semaphore_signal(barrier, inc=1, device_id=peer(6), device_id_type=MESH)
+
+    tok_rows = everyone.shape[1]
     top_k = ids_ref.shape[0]
     lines = info.shape[1] // 2
-    inner = lax.rem(lax.div(lax.div(blk, 2) + 1, 2), 2) == 1
+    for load_in in inputs:
+        load_in.wait()
     info[0] = jnp.full(info.shape[1:], -1.0, jnp.float32)
     info[0, :top_k] = ids_ref[...].astype(jnp.float32)
     info[0, lines:lines + top_k] = gates_ref[...]
-
-    barrier = pltpu.get_barrier_semaphore()
-    for device in (peer(2), peer(1), mate, across):
-        pl.semaphore_signal(barrier, inc=1, device_id=device, device_id_type=MESH)
-
-    @pl.when(inner)
-    def _():
-        pl.semaphore_signal(barrier, inc=1, device_id=peer(6), device_id_type=MESH)
-
     pl.semaphore_wait(barrier, 4 + jnp.where(inner, 1, 0))
 
     send(direct(2))
@@ -151,7 +162,6 @@
     def _():
         send(middle())
 
-    everyone[0] = tok_ref[...]
 
     def slots_of(m):
         square = (tok_rows, tok_rows)
@@ -247,14 +257,16 @@
                     near_copy(u, which).start()
 
     def join(u):
-        near_copy(u, 0).wait()
-        near_copy(u, 1).wait()
-        far_out[u] = (part[1, 1 - y] + near[u, 1 - y]).astype(jnp.bfloat16)
-        far_copy(u).start()
+        for which in range(2):
+            span = slice(which * cols, (which + 1) * cols)
+            near_copy(u, which).wait()
+            far_out[u, :, span] = (part[1, 1 - y, :, span] + near[u, 1 - y, :, span]).astype(jnp.bfloat16)
+            far_copy(u, which).start()
         near[u, y] = near[u, y] + part[1, y]
 
     def activate(u):
-        far_copy(u).wait()
+        far_copy(u, 0).wait()
+        far_copy(u, 1).wait()
         gate = near[u, y, :, :cols] + far_in[u, :, :cols].astype(jnp.float32)
         up = near[u, y, :, cols:] + far_in[u, :, cols:].astype(jnp.float32)
         hidden[u, c, y] = (gate / (1.0 + jnp.exp(-gate)) * up).astype(jnp.bfloat16)
@@ -353,11 +365,10 @@
     acc[...] = acc[...] + sum(arrived[m].astype(jnp.float32) for m in (2, 4, 6))
     for m in (1, 2, 4, 5, 6, 7):
         ret_copy(m).wait_send()
-    for m in (1, 3):
-        ret_copy(m).wait_recv()
-    out_ref[...] = (
-        acc[...] + arrived[1].astype(jnp.float32) + arrived[3].astype(jnp.float32)
-    ).astype(jnp.bfloat16)
+    ret_copy(1).wait_recv()
+    acc[...] = acc[...] + arrived[1].astype(jnp.float32)
+    ret_copy(3).wait_recv()
+    out_ref[...] = (acc[...] + arrived[3].astype(jnp.float32)).astype(jnp.bfloat16)
     ret_copy(3).wait_send()
 
 
@@ -371,13 +382,13 @@
     lines = top_k + -top_k % 8
     bf, f32 = jnp.bfloat16, jnp.float32
     dma = pltpu.SemaphoreType.DMA
-    counts = [n_blk + 1, n_blk, (2, 2), (2, 2)] + [RING] * 8 + [n_blk] * 2 + [n_blk + 1, n_blk]
+    counts = [n_blk + 1, n_blk, (2, 2), (2, 2)] + [(RING, 2)] * 2 + [RING] * 6 + [n_blk] * 2 + [n_blk + 1, n_blk]
     vmem = pl.BlockSpec(memory_space=pltpu.VMEM)
     anywhere = pl.BlockSpec(memory_space=pl.ANY)
     return pl.pallas_call(
         functools.partial(fused_kernel, n_blk),
         out_shape=pltpu.VMEM((tok_rows, width), bf),
-        in_specs=[vmem] * 3 + [anywhere] * 3,
+        in_specs=[anywhere] * 6,
         out_specs=vmem,
         scratch_shapes=[
             pltpu.VMEM(w_gate.shape, bf),
@@ -395,11 +406,13 @@
             pltpu.VMEM((n_blk, tok_rows, width), bf),
             pltpu.VMEM((n_blk // 2 - 2, tok_rows, width), f32),
             pltpu.VMEM((tok_rows, width), f32),
+            pltpu.VMEM((top_k, tok_rows), jnp.int32),
+            pltpu.VMEM((top_k, tok_rows), f32),
             pltpu.VMEM((n_blk, 2 * lines, tok_rows), f32),
             pltpu.VMEM((n_blk, held * capacity, tok_rows), bf),
             pltpu.VMEM((n_blk, held * capacity, tok_rows), bf),
             pltpu.VMEM((held, capacity, tok_rows), bf),
-            dma((5, 2)),
+            dma((6, 2)),
         ] + [dma(count if isinstance(count, tuple) else (count,)) for count in counts],
         compiler_params=pltpu.CompilerParams(
             collective_id=0, has_side_effects=True, vmem_limit_bytes=VMEM_BYTES

time: 102 us -> 101 us (level)
  Pallas kernels: 102 us -> 100 us
    pallas_call x1, Pallas kernels: 102 us -> 100 us  [fused(): pl.pallas_call(functools.partial(fused_kernel, n_blk), out_shape=pltpu.VM...]
where the time goes in v5:
time: 101 us
  Pallas kernels  100 us (99%)
    pallas_call x1, Pallas kernels, fused(): pl.pallas_call(functools.partial(fused_kernel, n_blk), out_shape=pltpu.VM...  100 us

profile of v5, /device:TPU:0, one launch (start us, length us, event | category | flops | bytes accessed | tf_op | source)
XLA Modules:
  0.0 101.0 jit_solution(7335171269035830808)
XLA Ops:
  0.0 100.2 %shard_map.64 = bf16[128,1280]{1,0:T(8,128)(2,1)S(1)} custom-call(bf16[128,1280]{1,0:T(8,128)(2,1)} %tok_hbm.1, s32[6,128]{1,0:T(8,128)} %bitcast.2, f32[6,128]{1,0:T(8,128)} %bitcast.3, bf16[2,1280,1536]{2,1,0:T(8,128)(2,1)} %wg_hbm.1, bf16[2,1280,1536]{2,1,0:T(8,128)(2,1)} %wu_hbm.1, bf16[2,1280,1536]{2,1,0:T(8,128)(2,1)} %wd_hbm.1), custom_call_target="tpu_custom_call" | custom-call | tf_op jit(solution)/shard_map/pallas_call | solution.py:388
  100.3 0.7 copy.8

commit v6 on v5

--- a/solution.py
+++ b/solution.py
@@ -12,6 +12,7 @@
 TILE = 384
 DOWN = 256
 RING = 4
+SPLIT = 512
 ORDER = (0, 2, 4, 5, 7, 6, 1, 3)
 
 
@@ -112,6 +113,15 @@
     def ret_copy(m):
         to = jnp.where((lax.rem(m, 2) == 1) & (m > 3), 1, m)
         return copy(outgoing.at[m], arrived.at[m], ret_s.at[m], ret_r.at[m], peer(to))
+
+    spans = ((0, SPLIT), (SPLIT, width))
+
+    def ret_part(m, k):
+        d0, d1 = spans[k]
+        sem = m if k == 0 else jnp.where(m == 1, 0, n_blk)
+        return copy(
+            outgoing.at[m, :, d0:d1], arrived.at[m, :, d0:d1], ret_s.at[sem], ret_r.at[sem], peer(m)
+        )
 
     def load(k, h):
         hbm, vmem = ((wg_hbm, wg), (wu_hbm, wu), (wd_hbm, wd))[k]
@@ -235,16 +245,15 @@
             load(2, 1).start()
 
         for side in range(2):
-            @pl.when(u == 0)
-            def _():
-                load_side(0, side).wait()
-                load_side(1, side).wait()
-                if side == 0:
-                    load(0, 1).start()
-                    load(1, 1).start()
-
             first = jnp.where(c == side, cols, 0)
             for which, w in enumerate((wg, wu)):
+                @pl.when(u == 0)
+                def _():
+                    load_side(which, side).wait()
+                    if side == 0 and which == 1:
+                        load(0, 1).start()
+                        load(1, 1).start()
+
                 for f in range(0, cols, TILE):
                     at = pl.multiple_of(first + f, 128)
                     got = jnp.dot(
@@ -288,20 +297,37 @@
         hidden_near(u).wait()
         hidden_onward(u).wait()
         rows = jnp.concatenate([hidden[u, k].reshape(cap, cols) for k in range(2)], axis=1)
-        for d in range(0, width, DOWN):
-            rows_out[h, :, d:d + DOWN] = lax.dot_general(
-                rows, wd[h, d:d + DOWN, :], (((1,), (1,)), ((), ())),
-                preferred_element_type=jnp.float32,
-            ).astype(jnp.bfloat16)
-
-        @pl.when(h == held - 1)
-        def _():
-            both = rows_out[...].reshape(held * cap, width)
+        def down(d0, d1):
+            for d in range(d0, d1, DOWN):
+                rows_out[h, :, d:d + DOWN] = lax.dot_general(
+                    rows, wd[h, d:d + DOWN, :], (((1,), (1,)), ((), ())),
+                    preferred_element_type=jnp.float32,
+                ).astype(jnp.bfloat16)
+
+        def mix(d0, d1):
+            both = rows_out[:, :, d0:d1].reshape(held * cap, d1 - d0)
             over_slots = (((0,), (0,)), ((), ()))
             mixed = lax.dot_general(high[m], both, over_slots, preferred_element_type=jnp.float32)
-            mixed = mixed + lax.dot_general(
+            return mixed + lax.dot_general(
                 low[m], both, over_slots, preferred_element_type=jnp.float32
             )
+
+        last = (m == 1) | (m == 3)
+
+        @pl.when((h < held - 1) | jnp.logical_not(last))
+        def _():
+            down(0, width)
+
+        @pl.when((h == held - 1) & last)
+        def _():
+            for k, (d0, d1) in enumerate(spans):
+                down(d0, d1)
+                outgoing[m, :, d0:d1] = mix(d0, d1).astype(jnp.bfloat16)
+                ret_part(m, k).start()
+
+        @pl.when((h == held - 1) & jnp.logical_not(last))
+        def _():
+            mixed = mix(0, width)
 
             @pl.when(m == 0)
             def _():
@@ -363,13 +389,18 @@
     for m in (2, 4, 6):
         ret_copy(m).wait_recv()
     acc[...] = acc[...] + sum(arrived[m].astype(jnp.float32) for m in (2, 4, 6))
-    for m in (1, 2, 4, 5, 6, 7):
+    for m in (2, 4, 5, 6, 7):
         ret_copy(m).wait_send()
-    ret_copy(1).wait_recv()
+    for k in range(2):
+        ret_part(1, k).wait_send()
+    for k in range(2):
+        ret_part(1, k).wait_recv()
     acc[...] = acc[...] + arrived[1].astype(jnp.float32)
-    ret_copy(3).wait_recv()
-    out_ref[...] = (acc[...] + arrived[3].astype(jnp.float32)).astype(jnp.bfloat16)
-    ret_copy(3).wait_send()
+    for k, (d0, d1) in enumerate(spans):
+        ret_part(3, k).wait_recv()
+        out_ref[:, d0:d1] = (acc[:, d0:d1] + arrived[3, :, d0:d1].astype(jnp.float32)).astype(jnp.bfloat16)
+    for k in range(2):
+        ret_part(3, k).wait_send()
 
 
 def fused(tokens, expert_ids, gate_vals, w_gate, w_up, w_down):
@@ -382,7 +413,7 @@
     lines = top_k + -top_k % 8
     bf, f32 = jnp.bfloat16, jnp.float32
     dma = pltpu.SemaphoreType.DMA
-    counts = [n_blk + 1, n_blk, (2, 2), (2, 2)] + [(RING, 2)] * 2 + [RING] * 6 + [n_blk] * 2 + [n_blk + 1, n_blk]
+    counts = [n_blk + 1, n_blk, (2, 2), (2, 2)] + [(RING, 2)] * 2 + [RING] * 6 + [n_blk + 1] * 3 + [n_blk]
     vmem = pl.BlockSpec(memory_space=pltpu.VMEM)
     anywhere = pl.BlockSpec(memory_space=pl.ANY)
     return pl.pallas_call(

time: 101 us -> 101 us (level)
  no operation moved by 1% of the time
where the time goes in v6:
time: 101 us
  Pallas kernels  99.9 us (99%)
    pallas_call x1, Pallas kernels, fused(): pl.pallas_call(functools.partial(fused_kernel, n_blk), out_shape=pltpu.VM...  99.9 us

profile of v6, /device:TPU:0, one launch (start us, length us, event | category | flops | bytes accessed | tf_op | source)
XLA Modules:
  0.0 100.6 jit_solution(17348370326130883071)
XLA Ops:
  0.0 99.9 %shard_map.64 = bf16[128,1280]{1,0:T(8,128)(2,1)S(1)} custom-call(bf16[128,1280]{1,0:T(8,128)(2,1)} %tok_hbm.1, s32[6,128]{1,0:T(8,128)} %bitcast.2, f32[6,128]{1,0:T(8,128)} %bitcast.3, bf16[2,1280,1536]{2,1,0:T(8,128)(2,1)} %wg_hbm.1, bf16[2,1280,1536]{2,1,0:T(8,128)(2,1)} %wu_hbm.1, bf16[2,1280,1536]{2,1,0:T(8,128)(2,1)} %wd_hbm.1), custom_call_target="tpu_custom_call" | custom-call | tf_op jit(solution)/shard_map/pallas_call | solution.py:419
  99.9 0.7 copy.8

commit v7 on v6

--- a/solution.py
+++ b/solution.py
@@ -307,10 +307,9 @@
         def mix(d0, d1):
             both = rows_out[:, :, d0:d1].reshape(held * cap, d1 - d0)
             over_slots = (((0,), (0,)), ((), ()))
-            mixed = lax.dot_general(high[m], both, over_slots, preferred_element_type=jnp.float32)
-            return mixed + lax.dot_general(
-                low[m], both, over_slots, preferred_element_type=jnp.float32
-            )
+            weights = jnp.concatenate([high[m], low[m]], axis=0)
+            twice = jnp.concatenate([both, both], axis=0)
+            return lax.dot_general(weights, twice, over_slots, preferred_element_type=jnp.float32)
 
         last = (m == 1) | (m == 3)
 

time: 101 us -> 101 us (level)
  no operation moved by 1% of the time
where the time goes in v7:
time: 101 us
  Pallas kernels  99.8 us (99%)
    pallas_call x1, Pallas kernels, fused(): pl.pallas_call(functools.partial(fused_kernel, n_blk), out_shape=pltpu.VM...  99.8 us

profile of v7, /device:TPU:0, one launch (start us, length us, event | category | flops | bytes accessed | tf_op | source)
XLA Modules:
  0.0 100.6 jit_solution(14530335825914995927)
XLA Ops:
  0.0 99.8 %shard_map.64 = bf16[128,1280]{1,0:T(8,128)(2,1)S(1)} custom-call(bf16[128,1280]{1,0:T(8,128)(2,1)} %tok_hbm.1, s32[6,128]{1,0:T(8,128)} %bitcast.2, f32[6,128]{1,0:T(8,128)} %bitcast.3, bf16[2,1280,1536]{2,1,0:T(8,128)(2,1)} %wg_hbm.1, bf16[2,1280,1536]{2,1,0:T(8,128)(2,1)} %wu_hbm.1, bf16[2,1280,1536]{2,1,0:T(8,128)(2,1)} %wd_hbm.1), custom_call_target="tpu_custom_call" | custom-call | tf_op jit(solution)/shard_map/pallas_call | solution.py:418
  99.8 0.7 copy.8
